TPU v7x, 32 devices: a whole 2x2x4 slice. The times are simulated.
32 devices in a mesh: mem: 4 (over x, core), reg: 8 (over z, y).
Axes of the slice: x: 2, y: 2, z: 4, core: 2. Of those that a mesh axis runs over, the one named last changes fastest.
Arguments:
- profiles: bfloat16 [2048, 80, 127], P('reg', 'mem'), may hold values from -6 to 6
- jacobian: bfloat16 [2048, 16, 127], P('reg'), may hold values from -0.5 to 0.5
- departure: float32 [32768], P('reg'), may hold values from -6 to 6
- obs_rinv: float32 [32768], P('reg'), may hold values from 0.1 to 2
- obs_level: int32 [32768], P('reg'), may hold values from 0 to 126
- vertical_modes: float32 [127, 12], replicated, may hold values from -2 to 2
- send_rows: int32 [8, 7, 512], P('reg'), may hold values from -1 to 4095, as said below
- counts: int32 [8, 7], P('reg'), may hold values from 64 to 512, as said below
- loc_taper: float32 [8, 7, 512], P('reg'), may hold values from 0.05 to 1
Outputs:
- gram_matrices: float32 [8, 960, 960], P('reg', 'mem')
- weighted_departures: float32 [8, 960], P('reg', 'mem')
Inputs may be any that keep to these rules, and one draw needn't show every extreme that they name: counts[s, d] of the 512 slots that owner s sends to region (s + d - 3) mod 8 are live, the first ones; in every draw one region has all 512 slots live from each of its 7 owners. `send_rows`: a live slot holds a row of the owner's 4096 observations, no row twice within one (s, d); the other slots hold -1.
All inputs are finite; a program needn't handle non-finite values.
Results may differ from a plain program's by a relative error of at most 0.0095.
Values may be sent and summed in bfloat16 or wider, within the bound.
A program may use at most 64 MiB of HBM per device.

v0:
```python
import functools

import jax
import jax.numpy as jnp
from jax import lax
from jax.experimental import pallas as pl
from jax.experimental.pallas import tpu as pltpu
from jax.sharding import PartitionSpec as P

ENS = 80
LANE = 128
GROUP = 16
NT = (((1,), (1,)), ((), ()))
VMEM = pl.BlockSpec(memory_space=pltpu.VMEM)
SMEM = pl.BlockSpec(memory_space=pltpu.SMEM)
MESH = pl.DeviceIdType.MESH
LAG = 2


def iota(shape, dim):
    return lax.broadcasted_iota(jnp.int32, shape, dim)


def hot(mask):
    return jnp.where(mask, 1.0, 0.0).astype(jnp.bfloat16)


def times(left, right):
    return jnp.dot(left, right, preferred_element_type=jnp.float32)


def split3(x):
    hi = x.astype(jnp.bfloat16).astype(jnp.float32)
    rest = x - hi
    mid = rest.astype(jnp.bfloat16).astype(jnp.float32)
    return hi, mid, rest - mid


def pick(
    order, ready, prof, jac, dep, rinv, level, modes, rows, counts, taper,
    out, wide, turned, extra, table, side, block,
):
    members, cols, levels = prof.shape
    channels = jac.shape[1]
    blocks, capacity = rows.shape[0], rows.shape[2]
    lanes = GROUP * channels
    his, height = table.shape[0], table.shape[1]
    share = side.shape[0] // lax.axis_size("mem")
    me = lax.axis_index("mem")

    depth = wide.shape[1] // channels
    for half in range(cols // LANE):
        part = jac[:, :, half * LANE : (half + 1) * LANE].reshape(levels * channels, LANE)
        wide[half, 0 : levels * channels, :] = part.astype(jnp.float32)
        for q in range(channels):
            plane = wide[half, pl.ds(q, depth, stride=channels), :]
            turned[q, half * LANE : (half + 1) * LANE, :] = plane.T[:, :levels].astype(jnp.bfloat16)

    extra[...] = jnp.zeros_like(extra)
    parts = split3(rinv[...]) + split3(dep[...]) + (level[...].astype(jnp.float32),)
    for k, part in enumerate(parts):
        for g in range(his):
            extra[g * 8 + k : g * 8 + k + 1, :] = part[:, g * lanes : (g + 1) * lanes]
    source, target = iota((lanes, lanes), 0), iota((lanes, lanes), 1)
    swap = hot(target == (source % channels) * GROUP + source // channels)
    extra[...] = times(extra[...].astype(jnp.bfloat16), swap)

    tall = members * GROUP
    diagonal = iota((tall, lanes), 0) % GROUP == iota((tall, lanes), 1) % GROUP
    fold = hot(iota((height, tall), 0) == iota((height, tall), 1) // GROUP)

    def fill(g, carry):
        first = pl.ds(pl.multiple_of(g * GROUP, GROUP), GROUP)
        left = prof[:, first, :].reshape(tall, levels)
        right = turned[:, first, :].reshape(lanes, levels)
        full = lax.dot_general(left, right, NT, preferred_element_type=jnp.float32)
        kept = jnp.where(diagonal, full, 0.0).astype(jnp.bfloat16)
        tail = extra[pl.ds(pl.multiple_of(g * 8, 8), 8), :]
        whole = jnp.concatenate([times(fold, kept)[: height - 8], tail], axis=0)
        table[g] = whole.astype(jnp.bfloat16)
        return carry

    lax.fori_loop(0, his, fill, 0, unroll=4)

    scaled = (modes[...] * ((ENS - 1) ** (-0.5))).astype(jnp.bfloat16)
    kinds = scaled.shape[0]
    side[...] = jnp.zeros_like(side)
    for k, d in enumerate(order):
        live = iota((1, capacity), 1) < counts[0, d]
        picked = jnp.where(live, rows[d], 0)
        high = picked // lanes
        low = (picked % channels) * GROUP + (picked // channels) % GROUP
        found = times(
            table[...].reshape(his * height, lanes), hot(iota((lanes, capacity), 0) == low)
        )
        chosen = jnp.where(high == 0, found[:height], 0.0)
        for h in range(1, his):
            chosen = jnp.where(high == h, found[h * height : (h + 1) * height], chosen)
        x = height - 8
        slot_rinv = chosen[x : x + 1] + chosen[x + 1 : x + 2] + chosen[x + 2 : x + 3]
        slot_dep = chosen[x + 3 : x + 4] + chosen[x + 4 : x + 5] + chosen[x + 5 : x + 6]
        slot_level = chosen[x + 6 : x + 7].astype(jnp.int32)
        weight32 = jnp.where(live, slot_rinv * taper[d], 0.0)
        side[0:1, :] = weight32
        side[1:2, :] = weight32 * slot_dep
        side[2 : 2 + kinds, :] = times(scaled, hot(iota((levels, capacity), 0) == slot_level))
        block[0:members, :] = chosen[0:members]
        for j in range(side.shape[0] // share):

            @pl.when(me == j)
            def _():
                block[members : members + share, :] = side[j * share : (j + 1) * share, :]

        out[d] = block[...].astype(jnp.bfloat16)
        ready(k)


def gram_kernel(
    members, kinds, share, prof, jac, dep, rinv, level, modes, rows, counts, taper, gram, depart,
    wide, turned, extra, table, side, block, mine, region, plain, weighted, dep_acc, s_reg, r_reg, s_x, r_x, s_p, r_p, s_q, r_q,
):
    blocks, height, capacity = mine.shape
    middle = blocks // 2
    n_mem, n_reg = lax.axis_size("mem"), lax.axis_size("reg")
    me, reg = lax.axis_index("mem"), lax.axis_index("reg")
    chips = n_mem // 2
    partner = {"mem": me + 1 - 2 * (me % 2), "reg": reg}

    def turn(k):
        k = blocks - 1 - k
        return middle + ((k + 1) // 2) * (1 - 2 * (k % 2))

    def to_reg(d):
        return {"mem": me, "reg": lax.rem(reg + d - middle + n_reg, n_reg)}

    def peer(j):
        return {"mem": lax.rem(me + 2 * j, n_mem), "reg": reg}

    def remote(src, dst, send, recv, device):
        return pltpu.make_async_remote_copy(
            src_ref=src, dst_ref=dst, send_sem=send, recv_sem=recv,
            device_id=device, device_id_type=MESH,
        )

    def across(d):
        return remote(mine.at[d], region.at[d, me], s_reg.at[d], r_reg.at[d], to_reg(d))

    def hop(d, j):
        at = region.at[d, me]
        return remote(at, at, s_x.at[d, j], r_x.at[d, j], peer(j))

    def hand(d):
        at = region.at[d, me]
        return remote(at, at, s_p.at[d], r_p.at[d], partner)

    def relay(d, j):
        at = region.at[d, lax.rem(me - 2 * j + n_mem, n_mem)]
        return remote(at, at, s_q.at[d, j], r_q.at[d, j], partner)

    barrier = pltpu.get_barrier_semaphore()
    greeted = [to_reg(turn(k)) for k in range(blocks - 1)] + [partner]
    greeted += [peer(j) for j in range(1, chips)]
    for device in greeted:
        pl.semaphore_signal(barrier, inc=1, device_id=device, device_id_type=MESH)

    def ready(k):
        if k == blocks - 1:
            region[middle, me] = mine[middle]
        if k == 1:
            pl.semaphore_wait(barrier, len(greeted))
        if k > 0:
            across(turn(k - 1)).start()

    pick(
        [turn(k) for k in range(blocks)], ready, prof, jac, dep, rinv, level, modes, rows, counts,
        taper, mine, wide, turned, extra, table, side, block,
    )
    gram[...] = jnp.zeros_like(gram)
    dep_acc[...] = jnp.zeros_like(dep_acc)
    size = members * kinds
    row, col = iota((size, height), 0), iota((size, height), 1)
    spread = hot(col == row // kinds)
    period = 4 * kinds
    line = iota((period, height), 0) % kinds + 2
    spot = iota((period, height), 1)
    spread_mode = [
        hot((line // share == j) & (spot == members + line % share)) for j in range(n_mem)
    ]

    def forward(k):
        d = turn(k)

        @pl.when(k < blocks - 1)
        def _():
            across(d).wait_recv()

        for j in range(1, chips):
            hop(d, j).start()
        hand(d).start()

    def pass_on(k):
        d = turn(k)
        for j in range(1, chips):
            hop(d, j).wait_recv()
            relay(d, j).start()

    def multiply(k):
        d = turn(k)
        hand(d).wait_recv()
        for j in range(1, chips):
            relay(d, j).wait_recv()
        mode = times(spread_mode[0], region[d, 0])
        for j in range(1, n_mem):
            mode += times(spread_mode[j], region[d, j])
        mode = jnp.concatenate([mode] * (size // period), axis=0)
        first = region[d, 0].astype(jnp.float32)
        weight, depw = first[members : members + 1], first[members + 1 : members + 2]
        for j in range(n_mem):
            z = (times(spread, region[d, j]) * mode).astype(jnp.bfloat16)
            plain[j] = z
            weighted[j * size : (j + 1) * size, :] = (z.astype(jnp.float32) * weight).astype(
                jnp.bfloat16
            )
        z_own = plain[me]
        gram[0] += lax.dot_general(z_own, weighted[...], NT, preferred_element_type=jnp.float32)
        dep16 = jnp.broadcast_to(depw, (16, capacity)).astype(jnp.bfloat16)
        dep_acc[...] += lax.dot_general(dep16, z_own, NT, preferred_element_type=jnp.float32)

    def step(k, carry):
        @pl.when(k < blocks)
        def _():
            forward(k)

        @pl.when((k >= LAG) & (k < blocks + LAG))
        def _():
            pass_on(k - LAG)

        @pl.when(k >= 2 * LAG)
        def _():
            multiply(k - 2 * LAG)

        return carry

    lax.fori_loop(0, blocks + 2 * LAG, step, 0)
    for k in range(blocks):
        d = turn(k)
        if k < blocks - 1:
            across(d).wait_send()
        hand(d).wait_send()
        for j in range(1, chips):
            hop(d, j).wait_send()
            relay(d, j).wait_send()
    depart[...] = dep_acc[0:1, :]


def local(
    profiles, jacobian, departure, obs_rinv, obs_level, vertical_modes, send_rows, counts, loc_taper
):
    cols, members, levels = profiles.shape
    channels = jacobian.shape[1]
    blocks, capacity = send_rows.shape[1], send_rows.shape[2]
    kinds = vertical_modes.shape[1]
    n_mem = lax.axis_size("mem")
    chips = n_mem // 2
    share = -(-(kinds + 2) // n_mem)
    height = members + share
    dma = pltpu.SemaphoreType.DMA
    own = members * kinds
    one, two = dma((blocks,)), dma((blocks, chips))
    gram, depart = pl.pallas_call(
        functools.partial(gram_kernel, members, kinds, share),
        out_shape=(
            jax.ShapeDtypeStruct((1, own, own * n_mem), jnp.float32),
            jax.ShapeDtypeStruct((1, own), jnp.float32),
        ),
        in_specs=[VMEM] * 7 + [SMEM, VMEM],
        out_specs=(VMEM, VMEM),
        scratch_shapes=[
            pltpu.VMEM((cols // LANE, -(-levels // LANE) * LANE * channels, LANE), jnp.float32),
            pltpu.VMEM((channels, cols, levels), jnp.bfloat16),
            pltpu.VMEM((cols // GROUP * 8, GROUP * channels), jnp.float32),
            pltpu.VMEM((cols // GROUP, 32, GROUP * channels), jnp.bfloat16),
            pltpu.VMEM((share * n_mem, capacity), jnp.float32),
            pltpu.VMEM((height, capacity), jnp.float32),
            pltpu.VMEM((blocks, height, capacity), jnp.bfloat16),
            pltpu.VMEM((blocks, n_mem, height, capacity), jnp.bfloat16),
            pltpu.VMEM((n_mem, own, capacity), jnp.bfloat16),
            pltpu.VMEM((own * n_mem, capacity), jnp.bfloat16),
            pltpu.VMEM((16, own), jnp.float32),
            one, one, two, two, one, one, two, two,
        ],
        compiler_params=pltpu.CompilerParams(collective_id=0, has_side_effects=True),
        name="gram",
    )(
        profiles.transpose(1, 0, 2), jacobian.transpose(2, 1, 0),
        departure[None], obs_rinv[None], obs_level[None], vertical_modes.T,
        send_rows.transpose(1, 0, 2), counts, loc_taper.transpose(1, 0, 2),
    )
    return gram, depart


def solution(mesh):
    in_specs = (
        P("reg", "mem", None),
        P("reg", None, None),
        P("reg"),
        P("reg"),
        P("reg"),
        P(),
        P("reg", None, None),
        P("reg", None),
        P("reg", None, None),
    )
    out_specs = (P("reg", "mem", None), P("reg", "mem"))
    return jax.shard_map(local, mesh=mesh, in_specs=in_specs, out_specs=out_specs, check_vma=False)
```

profile of v0, /device:TPU:0, one launch (start us, length us, event | category | flops | bytes accessed | tf_op | source)
XLA Modules:
  0.0 32.7 jit_solution(11940300204337876274)
XLA Ops:
  0.6 29.3 %gram.1 = (f32[1,240,960]{2,1,0:T(8,128)}, f32[1,240]{1,0:T(1,128)}) custom-call(bf16[20,256,127]{2,1,0:T(8,128)(2,1)} %bitcast.8, bf16[127,16,256]{2,1,0:T(8,128)(2,1)} %bitcast.9, f32[1,4096]{1,0:T(1,128)} %bitcast.10, f32[1,4096]{1,0:T(1,128)} %bitcast.11, s32[1,4096]{1,0:T(1,128)} %bitcast.12, f32[12,127]{1,0:T(8,128)} %bitcast.15, ...), custom_call_target="tpu_custom_call" | custom-call | tf_op jit(solution)/shard_map/gram/pallas_call | solution.py:270
  29.9 0.0 copy-start
  29.9 2.2 %copy.13 = f32[1,240,960]{2,1,0:T(8,128)} copy(f32[1,240,960]{2,1,0:T(8,128)} %get-tuple-element.4) | data formatting | bytes 1843200
  32.2 0.0 copy-done
  32.2 0.6 %copy.14 = f32[1,240]{1,0:T(1,128)} copy(f32[1,240]{1,0:T(1,128)S(1)} %copy-done) | data formatting | bytes 1920
Async XLA Ops:
  29.9 2.3 %copy-start = (f32[1,240]{1,0:T(1,128)S(1)}, f32[1,240]{1,0:T(1,128)}, u32[]{:S(2)}) copy-start(f32[1,240]{1,0:T(1,128)} %get-tuple-element.5) | copy-start | bytes 2884
where the time goes:
time: 32.9 us; the launch traced here: 32.7 us
  Pallas kernels  29.3 us (89%)
  local copies, waits for them, and re-layouts  2.81 us (9%)
  between operations  0.65 us (2%)
    pallas_call x1, Pallas kernels, local(): pl.pallas_call(functools.partial(gram_kernel, members, kinds, share), out...  29.3 us
    unnamed x4, local copies, waits for them, and re-layouts  2.81 us

commit v1 on v0

v1 whole, which is shorter than its diff:
```python
import functools

import jax
import jax.numpy as jnp
from jax import lax
from jax.experimental import pallas as pl
from jax.experimental.pallas import tpu as pltpu
from jax.sharding import PartitionSpec as P

ENS = 80
LANE = 128
SUB = 8
GROUP = 16
NT = (((1,), (1,)), ((), ()))
VMEM = pl.BlockSpec(memory_space=pltpu.VMEM)
HBM = pl.BlockSpec(memory_space=pltpu.MemorySpace.HBM)
MESH = pl.DeviceIdType.MESH


def iota(shape, dim):
    return lax.broadcasted_iota(jnp.int32, shape, dim)


def hot(mask):
    return jnp.where(mask, 1.0, 0.0).astype(jnp.bfloat16)


def times(left, right):
    return jnp.dot(left, right, preferred_element_type=jnp.float32)


def merge(a, b, bit, s, u):
    up = pltpu.roll(a, SUB - bit, 0)
    if b is None:
        return jnp.where((u & bit) != 0, up, a)
    low = (s & bit) == 0
    if 2 * bit == SUB:
        same = (s & bit) == (u & bit)
        return jnp.where(same, jnp.where(low, a, b), pltpu.roll(jnp.where(low, b, a), bit, 0))
    down = pltpu.roll(b, bit, 0)
    return jnp.where((u & bit) != 0, jnp.where(low, up, b), jnp.where(low, a, down))


def diagonal(parts, s, u):
    fours = [merge(parts[i], parts[i + 4] if len(parts) > 4 else None, 4, s, u) for i in range(4)]
    twos = [merge(fours[i], fours[i + 2], 2, s, u) for i in range(2)]
    return merge(twos[0], twos[1], 1, s, u)


def turn_jacobian(jac, wide, turned):
    levels, channels, cols = jac.shape
    pitch = wide.shape[1] // channels
    for l in range(levels):
        line = jac[l].astype(jnp.float32)
        for half in range(cols // LANE):
            for q in range(0, channels, SUB):
                part = line[q : q + SUB, half * LANE : (half + 1) * LANE]
                wide[half, pl.ds(q * pitch + l, SUB, stride=pitch), :] = part
    for half in range(cols // LANE):
        for q in range(channels):
            plane = wide[half, q * pitch : q * pitch + LANE, :]
            turned[q, half * LANE : (half + 1) * LANE, :] = plane.T[:, :levels].astype(jnp.bfloat16)


def side_rows(me, rinv, dep, level, modes, padded, extra, share):
    kinds, levels = modes.shape
    lanes = extra.shape[1]
    padded[...] = jnp.zeros_like(padded)
    padded[share : share + kinds, :] = modes[...] * ((ENS - 1) ** (-0.5))
    mine = padded[pl.ds(me * share, SUB), :].astype(jnp.bfloat16)
    s = iota((SUB, lanes), 0)
    holds_dep = (s == SUB - share + kinds % share) & (me == kinds // share)
    for g in range(extra.shape[0] // SUB):
        at = slice(g * lanes, (g + 1) * lanes)
        root = jnp.sqrt(rinv[:, at])
        high = root.astype(jnp.bfloat16).astype(jnp.float32)
        found = times(mine, hot(iota((levels, lanes), 0) == level[:, at]))
        found = jnp.where(holds_dep, dep[:, at] * root, found)
        found = jnp.where(s == 0, high, jnp.where(s == 1, root - high, found))
        extra[g * SUB : (g + 1) * SUB, :] = found
    channels = lanes // GROUP
    source, target = iota((lanes, lanes), 0), iota((lanes, lanes), 1)
    swap = hot(target == (source % channels) * GROUP + source // channels)
    extra[...] = times(extra[...].astype(jnp.bfloat16), swap)


def fill_table(prof, turned, extra, table):
    members, cols, levels = prof.shape
    groups, height, lanes = table.shape
    s, lane = iota((SUB, lanes), 0), iota((SUB, lanes), 1)
    u = lane % SUB
    upper = (lane // SUB) % 2 == 1

    def fill(g, carry):
        first = pl.ds(pl.multiple_of(g * GROUP, GROUP), GROUP)
        left = prof[:, first, :].reshape(members * GROUP, levels)
        right = turned[:, first, :].reshape(lanes, levels)
        full = lax.dot_general(left, right, NT, preferred_element_type=jnp.float32)
        parts = []
        for m in range(members):
            x = m * GROUP
            parts.append(jnp.where(upper, full[x + SUB : x + 2 * SUB], full[x : x + SUB]))
        more = extra[pl.ds(pl.multiple_of(g * SUB, SUB), SUB), :]
        root = more[0:1] + more[1:2]
        rows = [diagonal(parts[m : m + SUB], s, u) * root for m in range(0, members, SUB)]
        rows[-1] = jnp.where(s < members % SUB, rows[-1], more)
        table[g] = jnp.concatenate(rows, axis=0).astype(jnp.bfloat16)
        return carry

    lax.fori_loop(0, groups, fill, 0, unroll=4)


def gather_kernel(
    members, kinds, share, prof_h, jac_h, dep_h, rinv_h, level_h, modes_h, rows_h, counts_h, taper_h, acc,
    prof, jac, dep, rinv, level, modes, rows, counts, taper,
    padded, wide, turned, extra, table, picks, mine, region,
    s_in, s_reg, r_reg, s_hand, r_hand,
):
    blocks, height, capacity = mine.shape
    middle = blocks // 2
    n_mem, n_reg = lax.axis_size("mem"), lax.axis_size("reg")
    me, reg = lax.axis_index("mem"), lax.axis_index("reg")
    chips = n_mem // 2
    groups, _, lanes = table.shape
    channels = lanes // GROUP
    partner = {"mem": me + 1 - 2 * (me % 2), "reg": reg}
    pairs = [
        (level_h, level), (modes_h, modes), (rinv_h, rinv), (dep_h, dep), (rows_h, rows),
        (counts_h, counts), (taper_h, taper), (jac_h, jac), (prof_h, prof),
    ]
    loads = [pltpu.make_async_copy(h, v, s_in.at[i]) for i, (h, v) in enumerate(pairs)]
    for load in loads:
        load.start()

    def target(d, c):
        to = lax.rem(reg + d - middle + n_reg, n_reg)
        return {"mem": lax.rem(me + 2 * c, n_mem), "reg": to}

    def remote(src, dst, send, recv, device):
        return pltpu.make_async_remote_copy(
            src_ref=src, dst_ref=dst, send_sem=send, recv_sem=recv,
            device_id=device, device_id_type=MESH,
        )

    def across(d, c):
        return remote(mine.at[d], region.at[d, me], s_reg.at[d, c], r_reg.at[d, c], target(d, c))

    def hand(d, c):
        at = region.at[d, lax.rem(me - 2 * c + n_mem, n_mem)]
        return remote(at, at, s_hand.at[d, c], r_hand.at[d, c], partner)

    barrier = pltpu.get_barrier_semaphore()
    greeted = [target(d, c) for d in range(blocks) for c in range(chips) if (d, c) != (middle, 0)]
    greeted.append(partner)
    for device in greeted:
        pl.semaphore_signal(barrier, inc=1, device_id=device, device_id_type=MESH)

    at = lax.rem(middle - reg + n_reg, n_reg)
    lead = jnp.where(at < blocks, at, 0)

    def sent(k):
        return lax.rem(lead + k, blocks)

    def taken(k):
        return blocks - 1 - sent(k)

    for load in loads[:4]:
        load.wait()
    side_rows(me, rinv, dep, level, modes, padded, extra, share)
    for load in loads[4:7]:
        load.wait()

    def placed(d):
        live = iota((1, capacity), 1) < counts[0, d]
        return live, jnp.where(live, rows[d], 0)

    for d in range(blocks):
        _, picked = placed(d)
        low = (picked % channels) * GROUP + (picked // channels) % GROUP
        picks[d] = hot(iota((lanes, capacity), 0) == low)

    loads[7].wait()
    turn_jacobian(jac, wide, turned)
    loads[8].wait()
    fill_table(prof, turned, extra, table)

    s = iota((height, capacity), 0)
    is_dep = (s == members + kinds % share) & (me == kinds // share)
    for k in range(blocks):
        d = sent(k)
        live, picked = placed(d)
        high = picked // lanes
        found = times(table[...].reshape(groups * height, lanes), picks[d])
        chosen = found[:height]
        for h in range(1, groups):
            chosen = jnp.where(high == h, found[h * height : (h + 1) * height], chosen)
        root = jnp.sqrt(jnp.where(live, taper[d], 0.0))
        block = (chosen * jnp.where((s < members) | is_dep, root, 1.0)).astype(jnp.bfloat16)
        mine[d] = block
        if k == 0:
            pl.semaphore_wait(barrier, len(greeted))

        @pl.when(d == middle)
        def _():
            region[middle, me] = block

        @pl.when(d != middle)
        def _():
            across(d, 0).start()

        for c in range(1, chips):
            across(d, c).start()

    acc[...] = jnp.zeros_like(acc)
    size = members * kinds
    wide_rows = n_mem * height
    row, col = iota((2 * size, wide_rows), 0), iota((2 * size, wide_rows), 1)
    kind = row % kinds
    own = me * height + row // kinds
    spread = hot(col == jnp.where(row < size, own, (kind // share) * height + members + kind % share))

    def forward(k):
        d = taken(k)

        @pl.when(d != middle)
        def _():
            across(d, 0).wait_recv()

        hand(d, 0).start()
        for c in range(1, chips):
            across(d, c).wait_recv()
            hand(d, c).start()

    def multiply(k):
        d = taken(k)
        for c in range(chips):
            hand(d, c).wait_recv()
        parts = [region[d, j].astype(jnp.float32) for j in range(n_mem)]
        every = jnp.concatenate(parts, axis=0).astype(jnp.bfloat16)
        both = times(spread, every)
        own = (both[:size] * both[size:]).astype(jnp.bfloat16)
        lines = []
        for l in range(kinds):
            at = members + l % share
            line = jnp.broadcast_to(parts[l // share][at : at + 1], (GROUP, capacity))
            line = line.astype(jnp.bfloat16)
            lines.append(every * jnp.concatenate([line] * (wide_rows // GROUP), axis=0))
        lines.append(every[wide_rows - 2 * GROUP :])
        left = jnp.concatenate(lines, axis=0)
        acc[...] += lax.dot_general(left, own, NT, preferred_element_type=jnp.float32)

    def step(k, carry):
        @pl.when(k < blocks)
        def _():
            forward(k)

        @pl.when(k >= 1)
        def _():
            multiply(k - 1)

        return carry

    lax.fori_loop(0, blocks + 1, step, 0)
    for d in range(blocks):
        for c in range(chips):
            if (d, c) != (middle, 0):
                across(d, c).wait_send()
            hand(d, c).wait_send()


def write_kernel(members, kinds, n_mem, height, dep_row, acc, gram, depart, rows, out, out_dep, sems):
    size = members * kinds
    total = size * n_mem
    for t in range(-(-size // LANE)):
        wide = min(LANE, size - t * LANE)
        for l in range(kinds):
            for j in range(n_mem):
                at = (l * n_mem + j) * height
                part = acc[at : at + members, t * LANE : t * LANE + wide]
                to = pl.ds(j * size + l, members, stride=kinds)
                rows[t, to, 0:wide] = part
    out_dep[...] = acc[dep_row : dep_row + 1, :]
    pltpu.make_async_copy(out_dep, depart, sems.at[0]).start()
    copies = []
    for i in range(-(-total // LANE)):
        tall = min(LANE, total - i * LANE)
        at = slice(i * LANE, i * LANE + tall)
        for t in range(-(-size // LANE)):
            wide = min(LANE, size - t * LANE)
            turned = rows[t, at, :].T
            out[0, t * LANE : t * LANE + wide, at] = turned[:wide]
        copy = pltpu.make_async_copy(out.at[:, :, at], gram.at[:, :, at], sems.at[1 + i])
        copy.start()
        copies.append(copy)
    pltpu.make_async_copy(out_dep, depart, sems.at[0]).wait()
    for copy in copies:
        copy.wait()


def local(
    profiles, jacobian, departure, obs_rinv, obs_level, vertical_modes, send_rows, counts, loc_taper
):
    cols, members, levels = profiles.shape
    channels = jacobian.shape[1]
    blocks, capacity = send_rows.shape[1], send_rows.shape[2]
    kinds = vertical_modes.shape[1]
    n_mem = lax.axis_size("mem")
    chips = n_mem // 2
    share = -(-(kinds + 1) // n_mem)
    height = members + share
    size = members * kinds
    lanes = GROUP * channels
    dma = pltpu.SemaphoreType.DMA
    args = (
        profiles.transpose(1, 0, 2), jacobian.transpose(2, 1, 0),
        departure[None], obs_rinv[None], obs_level[None], vertical_modes.T,
        send_rows.transpose(1, 0, 2), counts, loc_taper.transpose(1, 0, 2),
    )
    args = [pltpu.with_memory_space_constraint(a, pltpu.MemorySpace.HBM) for a in args]
    buffers = [pltpu.VMEM(a.shape, a.dtype) for a in args]
    buffers[7] = pltpu.SMEM(counts.shape, counts.dtype)
    pitch = -(-levels // LANE) * LANE + 1
    acc_rows = kinds * n_mem * height + 2 * GROUP
    acc = pl.pallas_call(
        functools.partial(gather_kernel, members, kinds, share),
        out_shape=jax.ShapeDtypeStruct((acc_rows, size), jnp.float32),
        in_specs=[HBM] * 9,
        out_specs=VMEM,
        scratch_shapes=[
            *buffers,
            pltpu.VMEM((share * n_mem + SUB, levels), jnp.float32),
            pltpu.VMEM((cols // LANE, pitch * channels, LANE), jnp.float32),
            pltpu.VMEM((channels, cols, levels), jnp.bfloat16),
            pltpu.VMEM((cols // GROUP * SUB, lanes), jnp.float32),
            pltpu.VMEM((cols // GROUP, height, lanes), jnp.bfloat16),
            pltpu.VMEM((blocks, lanes, capacity), jnp.bfloat16),
            pltpu.VMEM((blocks, height, capacity), jnp.bfloat16),
            pltpu.VMEM((blocks, n_mem, height, capacity), jnp.bfloat16),
            dma((9,)), dma((blocks, chips)), dma((blocks, chips)), dma((blocks, chips)), dma((blocks, chips)),
        ],
        compiler_params=pltpu.CompilerParams(
            collective_id=0, has_side_effects=True, vmem_limit_bytes=32 << 20
        ),
        name="gather",
    )(*args)
    dep_row = kinds * n_mem * height + 2 * GROUP
    dep_row -= (n_mem - kinds // share) * height - members - kinds % share
    total = size * n_mem
    gram, depart = pl.pallas_call(
        functools.partial(write_kernel, members, kinds, n_mem, height, dep_row),
        out_shape=(
            jax.ShapeDtypeStruct((1, size, total), jnp.float32),
            jax.ShapeDtypeStruct((1, size), jnp.float32),
        ),
        in_specs=[VMEM],
        out_specs=(HBM, HBM),
        scratch_shapes=[
            pltpu.VMEM((-(-size // LANE), total, LANE), jnp.float32),
            pltpu.VMEM((1, size, total), jnp.float32),
            pltpu.VMEM((1, size), jnp.float32),
            dma((1 + -(-total // LANE),)),
        ],
        compiler_params=pltpu.CompilerParams(vmem_limit_bytes=16 << 20),
        name="write",
    )(acc)
    return gram, depart


def solution(mesh):
    in_specs = (
        P("reg", "mem", None),
        P("reg", None, None),
        P("reg"),
        P("reg"),
        P("reg"),
        P(),
        P("reg", None, None),
        P("reg", None),
        P("reg", None, None),
    )
    out_specs = (P("reg", "mem", None), P("reg", "mem"))
    return jax.shard_map(local, mesh=mesh, in_specs=in_specs, out_specs=out_specs, check_vma=False)
```

time: 32.9 us -> 22.4 us (0.68)
  the two profiles are of different devices: /device:TPU:0 before, /device:TPU:25 now
where the time goes in v1:
time: 22.4 us; the launch traced here: 22.1 us
  Pallas kernels  21.5 us (96%)
  between operations  0.64 us (3%)
    pallas_call x1, Pallas kernels, local(): pl.pallas_call(functools.partial(gather_kernel, members, kinds, share), o...  20.4 us
    pallas_call x1, Pallas kernels, local(): pl.pallas_call(functools.partial(write_kernel, members, kinds, n_mem, hei...  1.12 us

profile of v1, /device:TPU:25, one launch (start us, length us, event | category | flops | bytes accessed | tf_op | source)
XLA Modules:
  0.0 22.1 jit_solution(15790389418696969170)
XLA Ops:
  0.6 20.4 %gather.1.acc = f32[1184,240]{1,0:T(8,128)S(1)} custom-call(bf16[20,256,127]{2,1,0:T(8,128)(2,1)} %bitcast.8, bf16[127,16,256]{2,1,0:T(8,128)(2,1)} %bitcast.9, f32[1,4096]{1,0:T(1,128)} %bitcast.10, f32[1,4096]{1,0:T(1,128)} %bitcast.11, s32[1,4096]{1,0:T(1,128)} %bitcast.12, f32[12,127]{1,0:T(8,128)} %bitcast.15, s32[7,1,512]{2,1,0:T(1,128)} %bitcast.13, ...), custom_call_target="tpu_custom_call" | custom-call | tf_op jit(solution)/shard_map/gather/pallas_call | solution.py:324
  21.0 1.1 %write.1 = (f32[1,240,960]{2,1,0:T(8,128)}, f32[1,240]{1,0:T(1,128)}) custom-call(f32[1184,240]{1,0:T(8,128)S(1)} %gather.1.acc), custom_call_target="tpu_custom_call" | custom-call | tf_op jit(solution)/shard_map/write/pallas_call | solution.py:349

commit v2 on v1

--- a/solution.py
+++ b/solution.py
@@ -11,6 +11,9 @@
 LANE = 128
 SUB = 8
 GROUP = 16
+CROSS_REG = False
+CROSS_HOP = True
+LAG = 3
 NT = (((1,), (1,)), ((), ()))
 VMEM = pl.BlockSpec(memory_space=pltpu.VMEM)
 HBM = pl.BlockSpec(memory_space=pltpu.MemorySpace.HBM)
@@ -107,7 +110,7 @@
         table[g] = jnp.concatenate(rows, axis=0).astype(jnp.bfloat16)
         return carry
 
-    lax.fori_loop(0, groups, fill, 0, unroll=4)
+    lax.fori_loop(0, groups, fill, 0, unroll=16)
 
 
 def gather_kernel(
@@ -132,9 +135,22 @@
     for load in loads:
         load.start()
 
-    def target(d, c):
+    def other(x):
+        return x + 1 - 2 * lax.rem(x, 2)
+
+    def target(d):
         to = lax.rem(reg + d - middle + n_reg, n_reg)
-        return {"mem": lax.rem(me + 2 * c, n_mem), "reg": to}
+        return {"mem": other(me) if CROSS_REG else me, "reg": to}
+
+    def peer(c):
+        to = lax.rem(me + 2 * c, n_mem)
+        return other(to) if CROSS_HOP else to
+
+    def near(d, device):
+        return jnp.where(d == middle, device, other(device)) if CROSS_REG else device
+
+    def far(d, c):
+        return near(d, peer(chips - c))
 
     def remote(src, dst, send, recv, device):
         return pltpu.make_async_remote_copy(
@@ -142,16 +158,26 @@
             device_id=device, device_id_type=MESH,
         )
 
-    def across(d, c):
-        return remote(mine.at[d], region.at[d, me], s_reg.at[d, c], r_reg.at[d, c], target(d, c))
+    def across(d):
+        return remote(mine.at[d], region.at[d, me], s_reg.at[d, 0], r_reg.at[d, 0], target(d))
+
+    def hop(d, c):
+        at = region.at[d, near(d, me)]
+        to = {"mem": peer(c), "reg": reg}
+        return remote(at, at, s_reg.at[d, c], r_reg.at[d, c], to)
 
     def hand(d, c):
-        at = region.at[d, lax.rem(me - 2 * c + n_mem, n_mem)]
+        at = region.at[d, near(d, me) if c == 0 else far(d, c)]
         return remote(at, at, s_hand.at[d, c], r_hand.at[d, c], partner)
 
+    def spread_out(d):
+        for c in range(1, chips):
+            hop(d, c).start()
+        hand(d, 0).start()
+
     barrier = pltpu.get_barrier_semaphore()
-    greeted = [target(d, c) for d in range(blocks) for c in range(chips) if (d, c) != (middle, 0)]
-    greeted.append(partner)
+    greeted = [target(d) for d in range(blocks) if d != middle]
+    greeted += [partner] + [{"mem": peer(c), "reg": reg} for c in range(1, chips)]
     for device in greeted:
         pl.semaphore_signal(barrier, inc=1, device_id=device, device_id_type=MESH)
 
@@ -203,32 +229,33 @@
         @pl.when(d == middle)
         def _():
             region[middle, me] = block
+            spread_out(middle)
 
         @pl.when(d != middle)
         def _():
-            across(d, 0).start()
-
-        for c in range(1, chips):
-            across(d, c).start()
+            across(d).start()
 
     acc[...] = jnp.zeros_like(acc)
-    size = members * kinds
-    wide_rows = n_mem * height
-    row, col = iota((2 * size, wide_rows), 0), iota((2 * size, wide_rows), 1)
-    kind = row % kinds
-    own = me * height + row // kinds
-    spread = hot(col == jnp.where(row < size, own, (kind // share) * height + members + kind % share))
+    rows_of_eight = iota((SUB, capacity), 0)
+
+    def joined(first, second, rolled=False):
+        if not rolled:
+            second = pltpu.roll(second, share, 0)
+        seam = jnp.where(rows_of_eight < SUB - share, first[height - SUB :], second[:SUB])
+        return jnp.concatenate([first[: height - SUB], seam, second[SUB:]], axis=0)
 
     def forward(k):
         d = taken(k)
 
         @pl.when(d != middle)
         def _():
-            across(d, 0).wait_recv()
-
-        hand(d, 0).start()
+            across(d).wait_recv()
+            spread_out(d)
+
+    def pass_on(k):
+        d = taken(k)
         for c in range(1, chips):
-            across(d, c).wait_recv()
+            hop(d, c).wait_recv()
             hand(d, c).start()
 
     def multiply(k):
@@ -236,17 +263,25 @@
         for c in range(chips):
             hand(d, c).wait_recv()
         parts = [region[d, j].astype(jnp.float32) for j in range(n_mem)]
-        every = jnp.concatenate(parts, axis=0).astype(jnp.bfloat16)
-        both = times(spread, every)
-        own = (both[:size] * both[size:]).astype(jnp.bfloat16)
+        every = [joined(parts[j], parts[j + 1]) for j in range(0, n_mem, 2)]
+        every = jnp.concatenate(every, axis=0).astype(jnp.bfloat16)
+        low = region[d, me].astype(jnp.float32)
+        high = pltpu.roll(low, share, 0)
         lines = []
         for l in range(kinds):
             at = members + l % share
-            line = jnp.broadcast_to(parts[l // share][at : at + 1], (GROUP, capacity))
-            line = line.astype(jnp.bfloat16)
-            lines.append(every * jnp.concatenate([line] * (wide_rows // GROUP), axis=0))
-        lines.append(every[wide_rows - 2 * GROUP :])
-        left = jnp.concatenate(lines, axis=0)
+            lines.append(parts[l // share][at : at + 1])
+        own = []
+        for l in range(0, kinds, 2):
+            own.append(joined(low * lines[l], high * lines[l + 1], True))
+        own = jnp.concatenate(own, axis=0).astype(jnp.bfloat16)
+        left = []
+        for line in lines:
+            tall = jnp.broadcast_to(line, (GROUP, capacity)).astype(jnp.bfloat16)
+            left.append(every * jnp.concatenate([tall] * (every.shape[0] // GROUP), axis=0))
+        last = parts[kinds // share][height - SUB :]
+        left.append(jnp.concatenate([last, last], axis=0).astype(jnp.bfloat16))
+        left = jnp.concatenate(left, axis=0)
         acc[...] += lax.dot_general(left, own, NT, preferred_element_type=jnp.float32)
 
     def step(k, carry):
@@ -254,45 +289,56 @@
         def _():
             forward(k)
 
-        @pl.when(k >= 1)
-        def _():
-            multiply(k - 1)
+        @pl.when((k >= LAG) & (k < blocks + LAG))
+        def _():
+            pass_on(k - LAG)
+
+        @pl.when(k > LAG)
+        def _():
+            multiply(k - LAG - 1)
 
         return carry
 
-    lax.fori_loop(0, blocks + 1, step, 0)
+    lax.fori_loop(0, blocks + LAG + 1, step, 0)
     for d in range(blocks):
+        if d != middle:
+            across(d).wait_send()
+        for c in range(1, chips):
+            hop(d, c).wait_send()
         for c in range(chips):
-            if (d, c) != (middle, 0):
-                across(d, c).wait_send()
             hand(d, c).wait_send()
 
 
-def write_kernel(members, kinds, n_mem, height, dep_row, acc, gram, depart, rows, out, out_dep, sems):
+def write_kernel(members, kinds, n_mem, dep_row, acc, gram, depart, rows, lines, out, out_dep, sems):
     size = members * kinds
     total = size * n_mem
-    for t in range(-(-size // LANE)):
+    every = members * n_mem
+    tiles = -(-size // LANE)
+    for t in range(tiles):
         wide = min(LANE, size - t * LANE)
         for l in range(kinds):
-            for j in range(n_mem):
-                at = (l * n_mem + j) * height
-                part = acc[at : at + members, t * LANE : t * LANE + wide]
-                to = pl.ds(j * size + l, members, stride=kinds)
-                rows[t, to, 0:wide] = part
-    out_dep[...] = acc[dep_row : dep_row + 1, :]
-    pltpu.make_async_copy(out_dep, depart, sems.at[0]).start()
-    copies = []
+            part = acc[l * every : (l + 1) * every, t * LANE : t * LANE + wide]
+            rows[t, pl.ds(l, every, stride=kinds), 0:wide] = part
+    row, col = iota((size, size), 0), iota((size, size), 1)
+    swap = jnp.where(col == (row % members) * kinds + row // members, 1.0, 0.0)
+    out_dep[...] = jnp.dot(
+        acc[dep_row : dep_row + 1, :], swap, precision=lax.Precision.HIGHEST,
+        preferred_element_type=jnp.float32,
+    )
+    copies = [pltpu.make_async_copy(out_dep, depart, sems.at[0])]
+    copies[0].start()
     for i in range(-(-total // LANE)):
-        tall = min(LANE, total - i * LANE)
-        at = slice(i * LANE, i * LANE + tall)
-        for t in range(-(-size // LANE)):
-            wide = min(LANE, size - t * LANE)
-            turned = rows[t, at, :].T
-            out[0, t * LANE : t * LANE + wide, at] = turned[:wide]
+        at = slice(i * LANE, min(total, (i + 1) * LANE))
+        tall = at.stop - at.start
+        turned = [rows[t, at, :].T[: min(LANE, size - t * LANE)] for t in range(tiles)]
+        turned = jnp.concatenate(turned, axis=0)
+        for k in range(kinds):
+            part = turned[k * members : (k + 1) * members]
+            lines[i, pl.ds(k, members, stride=kinds), 0:tall] = part
+        out[0, :, at] = lines[i, :, 0:tall]
         copy = pltpu.make_async_copy(out.at[:, :, at], gram.at[:, :, at], sems.at[1 + i])
         copy.start()
         copies.append(copy)
-    pltpu.make_async_copy(out_dep, depart, sems.at[0]).wait()
     for copy in copies:
         copy.wait()
 
@@ -320,7 +366,7 @@
     buffers = [pltpu.VMEM(a.shape, a.dtype) for a in args]
     buffers[7] = pltpu.SMEM(counts.shape, counts.dtype)
     pitch = -(-levels // LANE) * LANE + 1
-    acc_rows = kinds * n_mem * height + 2 * GROUP
+    acc_rows = size * n_mem + GROUP
     acc = pl.pallas_call(
         functools.partial(gather_kernel, members, kinds, share),
         out_shape=jax.ShapeDtypeStruct((acc_rows, size), jnp.float32),
@@ -343,11 +389,10 @@
         ),
         name="gather",
     )(*args)
-    dep_row = kinds * n_mem * height + 2 * GROUP
-    dep_row -= (n_mem - kinds // share) * height - members - kinds % share
+    dep_row = size * n_mem + SUB - share + kinds % share
     total = size * n_mem
     gram, depart = pl.pallas_call(
-        functools.partial(write_kernel, members, kinds, n_mem, height, dep_row),
+        functools.partial(write_kernel, members, kinds, n_mem, dep_row),
         out_shape=(
             jax.ShapeDtypeStruct((1, size, total), jnp.float32),
             jax.ShapeDtypeStruct((1, size), jnp.float32),
@@ -356,6 +401,7 @@
         out_specs=(HBM, HBM),
         scratch_shapes=[
             pltpu.VMEM((-(-size // LANE), total, LANE), jnp.float32),
+            pltpu.VMEM((-(-total // LANE), size, LANE), jnp.float32),
             pltpu.VMEM((1, size, total), jnp.float32),
             pltpu.VMEM((1, size), jnp.float32),
             dma((1 + -(-total // LANE),)),

time: 22.4 us -> 20.3 us (0.906)
  the two profiles are of different devices: /device:TPU:25 before, /device:TPU:29 now
where the time goes in v2:
time: 20.3 us; the launch traced here: 20.1 us
  Pallas kernels  19.4 us (96%)
  between operations  0.64 us (3%)
    pallas_call x1, Pallas kernels, local(): pl.pallas_call(functools.partial(gather_kernel, members, kinds, share), o...  18.1 us
    pallas_call x1, Pallas kernels, local(): pl.pallas_call(functools.partial(write_kernel, members, kinds, n_mem, dep...  1.34 us

profile of v2, /device:TPU:29, one launch (start us, length us, event | category | flops | bytes accessed | tf_op | source)
XLA Modules:
  0.0 20.1 jit_solution(9692043241787509768)
XLA Ops:
  0.6 18.1 %gather.1.acc = f32[976,240]{1,0:T(8,128)S(1)} custom-call(bf16[20,256,127]{2,1,0:T(8,128)(2,1)} %bitcast.8, bf16[127,16,256]{2,1,0:T(8,128)(2,1)} %bitcast.9, f32[1,4096]{1,0:T(1,128)} %bitcast.10, f32[1,4096]{1,0:T(1,128)} %bitcast.11, s32[1,4096]{1,0:T(1,128)} %bitcast.12, f32[12,127]{1,0:T(8,128)} %bitcast.15, s32[7,1,512]{2,1,0:T(1,128)} %bitcast.13, ...), custom_call_target="tpu_custom_call" | custom-call | tf_op jit(solution)/shard_map/gather/pallas_call | solution.py:370
  18.7 1.3 %write.1 = (f32[1,240,960]{2,1,0:T(8,128)}, f32[1,240]{1,0:T(1,128)}) custom-call(f32[976,240]{1,0:T(8,128)S(1)} %gather.1.acc), custom_call_target="tpu_custom_call" | custom-call | tf_op jit(solution)/shard_map/write/pallas_call | solution.py:394

commit v3 on v2

--- a/solution.py
+++ b/solution.py
@@ -13,7 +13,7 @@
 GROUP = 16
 CROSS_REG = False
 CROSS_HOP = True
-LAG = 3
+LAG = 4
 NT = (((1,), (1,)), ((), ()))
 VMEM = pl.BlockSpec(memory_space=pltpu.VMEM)
 HBM = pl.BlockSpec(memory_space=pltpu.MemorySpace.HBM)
@@ -293,13 +293,13 @@
         def _():
             pass_on(k - LAG)
 
-        @pl.when(k > LAG)
-        def _():
-            multiply(k - LAG - 1)
+        @pl.when(k >= LAG + 2)
+        def _():
+            multiply(k - LAG - 2)
 
         return carry
 
-    lax.fori_loop(0, blocks + LAG + 1, step, 0)
+    lax.fori_loop(0, blocks + LAG + 2, step, 0)
     for d in range(blocks):
         if d != middle:
             across(d).wait_send()

time: 20.3 us -> 19.4 us (0.956)
  the two profiles are of different devices: /device:TPU:29 before, /device:TPU:25 now
where the time goes in v3:
time: 19.4 us; the launch traced here: 19.1 us
  Pallas kernels  18.5 us (95%)
  between operations  0.64 us (3%)
    pallas_call x1, Pallas kernels, local(): pl.pallas_call(functools.partial(gather_kernel, members, kinds, share), o...  17.2 us
    pallas_call x1, Pallas kernels, local(): pl.pallas_call(functools.partial(write_kernel, members, kinds, n_mem, dep...  1.34 us

profile of v3, /device:TPU:25, one launch (start us, length us, event | category | flops | bytes accessed | tf_op | source)
XLA Modules:
  0.0 19.1 jit_solution(16766398831175309013)
XLA Ops:
  0.6 17.2 %gather.1.acc = f32[976,240]{1,0:T(8,128)S(1)} custom-call(bf16[20,256,127]{2,1,0:T(8,128)(2,1)} %bitcast.8, bf16[127,16,256]{2,1,0:T(8,128)(2,1)} %bitcast.9, f32[1,4096]{1,0:T(1,128)} %bitcast.10, f32[1,4096]{1,0:T(1,128)} %bitcast.11, s32[1,4096]{1,0:T(1,128)} %bitcast.12, f32[12,127]{1,0:T(8,128)} %bitcast.15, s32[7,1,512]{2,1,0:T(1,128)} %bitcast.13, ...), custom_call_target="tpu_custom_call" | custom-call | tf_op jit(solution)/shard_map/gather/pallas_call | solution.py:370
  17.8 1.3 %write.1 = (f32[1,240,960]{2,1,0:T(8,128)}, f32[1,240]{1,0:T(1,128)}) custom-call(f32[976,240]{1,0:T(8,128)S(1)} %gather.1.acc), custom_call_target="tpu_custom_call" | custom-call | tf_op jit(solution)/shard_map/write/pallas_call | solution.py:394

commit v4 on v3

--- a/solution.py
+++ b/solution.py
@@ -116,7 +116,7 @@
 def gather_kernel(
     members, kinds, share, prof_h, jac_h, dep_h, rinv_h, level_h, modes_h, rows_h, counts_h, taper_h, acc,
     prof, jac, dep, rinv, level, modes, rows, counts, taper,
-    padded, wide, turned, extra, table, picks, mine, region,
+    padded, wide, turned, extra, table, mine, region,
     s_in, s_reg, r_reg, s_hand, r_hand,
 ):
     blocks, height, capacity = mine.shape
@@ -187,8 +187,10 @@
     def sent(k):
         return lax.rem(lead + k, blocks)
 
+    late = 4 * reg >= 3 * n_reg
+
     def taken(k):
-        return blocks - 1 - sent(k)
+        return blocks - 1 - lax.rem(lead + jnp.where(late, blocks - 1 - k, k), blocks)
 
     for load in loads[:4]:
         load.wait()
@@ -199,11 +201,6 @@
     def placed(d):
         live = iota((1, capacity), 1) < counts[0, d]
         return live, jnp.where(live, rows[d], 0)
-
-    for d in range(blocks):
-        _, picked = placed(d)
-        low = (picked % channels) * GROUP + (picked // channels) % GROUP
-        picks[d] = hot(iota((lanes, capacity), 0) == low)
 
     loads[7].wait()
     turn_jacobian(jac, wide, turned)
@@ -216,7 +213,8 @@
         d = sent(k)
         live, picked = placed(d)
         high = picked // lanes
-        found = times(table[...].reshape(groups * height, lanes), picks[d])
+        low = (picked % channels) * GROUP + (picked // channels) % GROUP
+        found = times(table[...].reshape(groups * height, lanes), hot(iota((lanes, capacity), 0) == low))
         chosen = found[:height]
         for h in range(1, groups):
             chosen = jnp.where(high == h, found[h * height : (h + 1) * height], chosen)
@@ -314,31 +312,39 @@
     total = size * n_mem
     every = members * n_mem
     tiles = -(-size // LANE)
-    for t in range(tiles):
-        wide = min(LANE, size - t * LANE)
-        for l in range(kinds):
-            part = acc[l * every : (l + 1) * every, t * LANE : t * LANE + wide]
-            rows[t, pl.ds(l, every, stride=kinds), 0:wide] = part
-    row, col = iota((size, size), 0), iota((size, size), 1)
-    swap = jnp.where(col == (row % members) * kinds + row // members, 1.0, 0.0)
-    out_dep[...] = jnp.dot(
-        acc[dep_row : dep_row + 1, :], swap, precision=lax.Precision.HIGHEST,
-        preferred_element_type=jnp.float32,
-    )
-    copies = [pltpu.make_async_copy(out_dep, depart, sems.at[0])]
-    copies[0].start()
-    for i in range(-(-total // LANE)):
-        at = slice(i * LANE, min(total, (i + 1) * LANE))
-        tall = at.stop - at.start
-        turned = [rows[t, at, :].T[: min(LANE, size - t * LANE)] for t in range(tiles)]
-        turned = jnp.concatenate(turned, axis=0)
-        for k in range(kinds):
-            part = turned[k * members : (k + 1) * members]
-            lines[i, pl.ds(k, members, stride=kinds), 0:tall] = part
-        out[0, :, at] = lines[i, :, 0:tall]
-        copy = pltpu.make_async_copy(out.at[:, :, at], gram.at[:, :, at], sems.at[1 + i])
-        copy.start()
-        copies.append(copy)
+    copies = []
+    done = 0
+    for first in range(0, every, GROUP):
+        count = min(GROUP, every - first)
+        for t in range(tiles):
+            wide = min(LANE, size - t * LANE)
+            for l in range(kinds):
+                at = l * every + first
+                to = pl.ds(first * kinds + l, count, stride=kinds)
+                rows[t, to, 0:wide] = acc[at : at + count, t * LANE : t * LANE + wide]
+        filled = (first + count) * kinds
+        while done < total and min(done + LANE, total) <= filled:
+            at = slice(done, min(total, done + LANE))
+            i, tall = done // LANE, at.stop - done
+            turned = [rows[t, at, :].T[: min(LANE, size - t * LANE)] for t in range(tiles)]
+            turned = jnp.concatenate(turned, axis=0)
+            for k in range(kinds):
+                part = turned[k * members : (k + 1) * members]
+                lines[i, pl.ds(k, members, stride=kinds), 0:tall] = part
+            out[0, :, at] = lines[i, :, 0:tall]
+            copy = pltpu.make_async_copy(out.at[:, :, at], gram.at[:, :, at], sems.at[1 + i])
+            copy.start()
+            copies.append(copy)
+            done += LANE
+        if first == 0:
+            row, col = iota((size, size), 0), iota((size, size), 1)
+            swap = jnp.where(col == (row % members) * kinds + row // members, 1.0, 0.0)
+            out_dep[...] = jnp.dot(
+                acc[dep_row : dep_row + 1, :], swap, precision=lax.Precision.HIGHEST,
+                preferred_element_type=jnp.float32,
+            )
+            copies.append(pltpu.make_async_copy(out_dep, depart, sems.at[0]))
+            copies[-1].start()
     for copy in copies:
         copy.wait()
 
@@ -379,7 +385,6 @@
             pltpu.VMEM((channels, cols, levels), jnp.bfloat16),
             pltpu.VMEM((cols // GROUP * SUB, lanes), jnp.float32),
             pltpu.VMEM((cols // GROUP, height, lanes), jnp.bfloat16),
-            pltpu.VMEM((blocks, lanes, capacity), jnp.bfloat16),
             pltpu.VMEM((blocks, height, capacity), jnp.bfloat16),
             pltpu.VMEM((blocks, n_mem, height, capacity), jnp.bfloat16),
             dma((9,)), dma((blocks, chips)), dma((blocks, chips)), dma((blocks, chips)), dma((blocks, chips)),

time: 19.4 us -> 18.9 us (0.974)
  Pallas kernels: 18.5 us -> 18 us
    pallas_call x1, Pallas kernels: 17.2 us -> 16.7 us  [local(): pl.pallas_call(functools.partial(gather_kernel, members, kinds, share), o...]
where the time goes in v4:
time: 18.9 us; the launch traced here: 18.7 us
  Pallas kernels  18 us (95%)
  between operations  0.64 us (3%)
    pallas_call x1, Pallas kernels, local(): pl.pallas_call(functools.partial(gather_kernel, members, kinds, share), o...  16.7 us
    pallas_call x1, Pallas kernels, local(): pl.pallas_call(functools.partial(write_kernel, members, kinds, n_mem, dep...  1.31 us

profile of v4, /device:TPU:25, one launch (start us, length us, event | category | flops | bytes accessed | tf_op | source)
XLA Modules:
  0.0 18.7 jit_solution(17559729660886241886)
XLA Ops:
  0.6 16.7 %gather.1.acc = f32[976,240]{1,0:T(8,128)S(1)} custom-call(bf16[20,256,127]{2,1,0:T(8,128)(2,1)} %bitcast.8, bf16[127,16,256]{2,1,0:T(8,128)(2,1)} %bitcast.9, f32[1,4096]{1,0:T(1,128)} %bitcast.10, f32[1,4096]{1,0:T(1,128)} %bitcast.11, s32[1,4096]{1,0:T(1,128)} %bitcast.12, f32[12,127]{1,0:T(8,128)} %bitcast.15, s32[7,1,512]{2,1,0:T(1,128)} %bitcast.13, ...), custom_call_target="tpu_custom_call" | custom-call | tf_op jit(solution)/shard_map/gather/pallas_call | solution.py:376
  17.3 1.3 %write.1 = (f32[1,240,960]{2,1,0:T(8,128)}, f32[1,240]{1,0:T(1,128)}) custom-call(f32[976,240]{1,0:T(8,128)S(1)} %gather.1.acc), custom_call_target="tpu_custom_call" | custom-call | tf_op jit(solution)/shard_map/write/pallas_call | solution.py:399

commit v5 on v4

--- a/solution.py
+++ b/solution.py
@@ -185,12 +185,15 @@
     lead = jnp.where(at < blocks, at, 0)
 
     def sent(k):
-        return lax.rem(lead + k, blocks)
+        return lax.rem(lead + jnp.where(2 * reg < n_reg, jnp.where(k < 2, k, blocks + 1 - k), k), blocks)
 
     late = 4 * reg >= 3 * n_reg
 
+    home = lax.rem(middle - lead + blocks, blocks)
+
     def taken(k):
-        return blocks - 1 - lax.rem(lead + jnp.where(late, blocks - 1 - k, k), blocks)
+        first = jnp.where(k == 0, home, jnp.where(k <= home, k - 1, k))
+        return blocks - 1 - lax.rem(lead + jnp.where(late, blocks - 1 - k, first), blocks)
 
     for load in loads[:4]:
         load.wait()

time: 18.9 us -> 18.8 us (level)
  no operation moved by 1% of the time
where the time goes in v5:
time: 18.8 us; the launch traced here: 18.6 us
  Pallas kernels  17.9 us (95%)
  between operations  0.64 us (3%)
    pallas_call x1, Pallas kernels, local(): pl.pallas_call(functools.partial(gather_kernel, members, kinds, share), o...  16.6 us
    pallas_call x1, Pallas kernels, local(): pl.pallas_call(functools.partial(write_kernel, members, kinds, n_mem, dep...  1.31 us

profile of v5, /device:TPU:25, one launch (start us, length us, event | category | flops | bytes accessed | tf_op | source)
XLA Modules:
  0.0 18.6 jit_solution(4839399935524883508)
XLA Ops:
  0.6 16.6 %gather.1.acc = f32[976,240]{1,0:T(8,128)S(1)} custom-call(bf16[20,256,127]{2,1,0:T(8,128)(2,1)} %bitcast.8, bf16[127,16,256]{2,1,0:T(8,128)(2,1)} %bitcast.9, f32[1,4096]{1,0:T(1,128)} %bitcast.10, f32[1,4096]{1,0:T(1,128)} %bitcast.11, s32[1,4096]{1,0:T(1,128)} %bitcast.12, f32[12,127]{1,0:T(8,128)} %bitcast.15, s32[7,1,512]{2,1,0:T(1,128)} %bitcast.13, ...), custom_call_target="tpu_custom_call" | custom-call | tf_op jit(solution)/shard_map/gather/pallas_call | solution.py:379
  17.3 1.3 %write.1 = (f32[1,240,960]{2,1,0:T(8,128)}, f32[1,240]{1,0:T(1,128)}) custom-call(f32[976,240]{1,0:T(8,128)S(1)} %gather.1.acc), custom_call_target="tpu_custom_call" | custom-call | tf_op jit(solution)/shard_map/write/pallas_call | solution.py:402
